TPU v7x, 32 devices: a whole 2x2x4 slice. The times are simulated.
32 devices in a mesh: tm: 8 (over y, x, core), sr: 4 (over z).
Axes of the slice: x: 2, y: 2, z: 4, core: 2. Of those that a mesh axis runs over, the one named last changes fastest.
Arguments:
- observations: bfloat16 [1024, 65536], P(None, ('sr', 'tm')), may hold values from -6 to 6
- loadings: float32 [65536, 128], P(('sr', 'tm')), may hold values from -0.0007324219 to 0.0007324219
- noise_precision: float32 [65536], P(('sr', 'tm')), may hold values from 0.5 to 4
- transition: float32 [128, 128], replicated, may hold values from -1 to 1, as said below
- filter_cov: float32 [128, 128], replicated, may hold values from -1 to 1, as said below
- smoother_gain: float32 [128, 128], replicated, may hold values from -1 to 1, as said below
- smoothed_cov: float32 [128, 128], replicated, may hold values from -1 to 1, as said below
Outputs:
- smoothed_factors: float32 [1024, 128], P('tm')
- new_loadings: float32 [65536, 128], P(('sr', 'tm'))
- new_transition: float32 [128, 128], replicated
Inputs may be any that keep to these rules, and one draw needn't show every extreme that they name: `transition`: the spectral radius is below one. `filter_cov`: symmetric positive definite. `smoother_gain`: the spectral radius is below one. `smoothed_cov`: symmetric positive definite.
All inputs are finite; a program needn't handle non-finite values.
Results may differ from a plain program's by a relative error of at most 0.00175.
The roundings to bfloat16 on the way count: a program that leaves them out, or rounds other values in their place, can miss the bound.
Values may be sent and summed in bfloat16 or wider, within the bound.
A program may use at most 64 MiB of HBM per device.

v0:
```python
import jax
import jax.numpy as jnp
from jax import lax
from jax.sharding import PartitionSpec as P

precise = lax.Precision.HIGHEST


def carried_in(part, axis, combine, identity, reverse):
    count = lax.axis_size(axis)
    place = lax.axis_index(axis)
    ahead = count - 1 - place if reverse else place
    gathered = jax.tree.map(lambda a: lax.all_gather(a, axis), part)
    state = jax.tree.map(lambda a, e: jnp.zeros_like(a) + jnp.asarray(e, a.dtype), part, identity)

    def one(hop, state):
        source = count - 1 - hop if reverse else hop
        return combine(
            state, jax.tree.map(lambda a: lax.dynamic_index_in_dim(a, source, 0, False), gathered)
        )

    return lax.fori_loop(0, ahead, one, state)


def shifted(value, axis, steps):
    count = lax.axis_size(axis)
    leading, last = (max(0, -steps), min(count, count - steps))
    return lax.ppermute(value, axis, [(source, source + steps) for source in range(leading, last)])


def dot_high(left, right):
    return jnp.dot(left, right, precision=precise, preferred_element_type=jnp.float32)


def matrix_power(matrix, exponent):
    result = jnp.eye(matrix.shape[0], dtype=jnp.float32)
    square = matrix
    remain = exponent
    while remain > 0:
        if remain % 2 == 1:
            result = dot_high(result, square)
        remain = remain // 2
        if remain > 0:
            square = dot_high(square, square)
    return result


def block_prefix(inputs, matrix):
    length = inputs.shape[0]
    width = inputs.shape[1]
    totals = inputs
    raised = matrix
    offset = 1
    while offset < length:
        moved = jnp.concatenate(
            [jnp.zeros((offset, width), jnp.float32), totals[: length - offset]], axis=0
        )
        totals = totals + dot_high(moved, raised.T)
        offset = offset * 2
        if offset < length:
            raised = dot_high(raised, raised)
    return totals


def propagate(start, matrix, length):
    carried = dot_high(matrix, start)[None, :]
    raised = matrix
    while carried.shape[0] < length:
        carried = jnp.concatenate([carried, dot_high(carried, raised.T)], axis=0)
        raised = dot_high(raised, raised)
    return carried


def compose(earlier, later):
    return (dot_high(later[0], earlier[0]), dot_high(later[0], earlier[1]) + later[1])


def local(
    observations, loadings, noise_precision, transition, filter_cov, smoother_gain, smoothed_cov
):
    blocks = lax.axis_size("tm")
    position = lax.axis_index("tm")
    width = transition.shape[0]
    steps_dev = observations.shape[0] // blocks
    scaled = (noise_precision[:, None] * loadings).astype(jnp.bfloat16)
    window = observations
    partial_value = lax.psum_scatter(
        jnp.dot(window, scaled, preferred_element_type=jnp.float32),
        "tm",
        scatter_dimension=0,
        tiled=True,
    )
    info_part = dot_high(loadings.T, noise_precision[:, None] * loadings)
    proj = lax.psum(partial_value, "sr")
    info = lax.psum(info_part, ("tm", "sr"))
    closed = transition - dot_high(filter_cov, dot_high(info, transition))
    inputs = dot_high(proj, filter_cov.T)
    local_filter = block_prefix(inputs, closed)
    whole_filter = matrix_power(closed, steps_dev)
    identity_pair = (jnp.eye(width, dtype=jnp.float32), jnp.zeros((width,), jnp.float32))
    entering = carried_in(
        (whole_filter, local_filter[steps_dev - 1]), "tm", compose, identity_pair, False
    )[1]
    filtered = local_filter + propagate(entering, closed, steps_dev)
    coupled = dot_high(smoother_gain, transition)
    global_rows = position * steps_dev + jnp.arange(steps_dev, dtype=jnp.int32)
    final_row = (global_rows == steps_dev * blocks - 1)[:, None]
    back = jnp.where(final_row, filtered, filtered - dot_high(filtered, coupled.T))
    local_smooth = block_prefix(back[::-1], smoother_gain)[::-1]
    whole_smooth = matrix_power(smoother_gain, steps_dev)
    arriving = carried_in((whole_smooth, local_smooth[0]), "tm", compose, identity_pair, True)[1]
    smoothed = local_smooth + propagate(arriving, smoother_gain, steps_dev)[::-1]
    factors_b = smoothed.astype(jnp.bfloat16)
    prior_row = shifted(smoothed[steps_dev - 1 :], "tm", 1)
    lag_rows = jnp.concatenate([prior_row, smoothed[: steps_dev - 1]], axis=0)
    kept_rows = jnp.where(final_row, 0.0, smoothed)
    total_part = dot_high(smoothed.T, smoothed)
    previous_part = dot_high(kept_rows.T, kept_rows)
    lagged_part = dot_high(smoothed.T, lag_rows)
    total, previous, lagged = lax.psum((total_part, previous_part, lagged_part), "tm")
    length = steps_dev * blocks
    total = total + length * smoothed_cov
    previous = previous + (length - 1) * smoothed_cov
    lagged = lagged + (length - 1) * dot_high(smoothed_cov, smoother_gain.T)
    window = observations
    cross = jnp.einsum(
        "ts,tk->sk",
        window,
        lax.all_gather(factors_b, "tm", axis=0, tiled=True),
        preferred_element_type=jnp.float32,
    )
    total_factor = jnp.linalg.cholesky(total)
    new_loadings = jax.scipy.linalg.cho_solve((total_factor, True), cross.T).T
    previous_factor = jnp.linalg.cholesky(previous)
    new_transition = jax.scipy.linalg.cho_solve((previous_factor, True), lagged.T).T
    return (smoothed, new_loadings, new_transition)


def solution(mesh):
    in_specs = (P(None, ("sr", "tm")), P(("sr", "tm"), None), P(("sr", "tm")), P(), P(), P(), P())
    out_specs = (P("tm", None), P(("sr", "tm"), None), P())
    return jax.shard_map(local, mesh=mesh, in_specs=in_specs, out_specs=out_specs, check_vma=False)
```

profile of v0, /device:TPU:0, one launch (start us, length us, event | category | flops | bytes accessed | tf_op | source)
XLA Modules:
  0.0 331.9 jit_solution(2547815003200978211)
XLA Ops:
  8.1 4.4 %fusion.13 = f32[128,128]{0,1:T(8,128)} fusion(f32[2048,128]{1,0:T(8,128)} %param.13, f32[2048]{0:T(1024)} %param.14), kind=kOutput, calls=%fused_computation.18 | convolution fusion | flops 402915328 | bytes 1122304 | tf_op jit(solution)/shard_map/dot_general | solution.py:32
  12.6 5.3 %convolution_bitcast_fusion.2 = f32[1024,128]{0,1:T(8,128)} fusion(bf16[1024,2048]{1,0:T(8,128)(2,1)} %param.12, f32[2048,128]{1,0:T(8,128)} %param.13, f32[2048]{0:T(1024)} %param.14), kind=kOutput, calls=%fused_computation.15 | convolution fusion | flops 537395200 | bytes 5775360 | tf_op jit(solution)/shard_map/dot_general | solution.py:88
  18.0 0.2 fusion.136
  18.6 0.3 convolution_multiply_fusion
  20.3 11.4 %all-gather.1 = f32[1024,128]{1,0:T(8,128)S(1)} all-gather(f32[128,128]{1,0:T(8,128)S(1)} %fusion.46), channel_id=3, replica_groups=mesh['tm'=8,'sr'=4] {'tm'}, dimensions={0}, use_global_device_ids=true | all-gather | bytes 589824 | tf_op jit(solution)/shard_map/all_gather | solution.py:13
  31.7 105.7 %all-reduce.21.cloned.1.call-done = f32[128,128]{0,1:T(8,128)} async-done(((f32[128,128]{0,1:T(8,128)}), f32[128,128]{0,1:T(8,128)}) %all-reduce.21.cloned.1.call-update) | async-done | bytes 65552 | tf_op jit(solution)/shard_map/psum | solution.py:95
  137.3 1.1 fusion.125
  138.5 0.3 fusion.16
  138.8 0.3 fusion.126
  140.6 10.4 %all-gather = f32[1024,128]{1,0:T(8,128)S(1)} all-gather(f32[128,128]{1,0:T(8,128)S(1)} %fusion.47), channel_id=2, replica_groups=mesh['tm'=8,'sr'=4] {'tm'}, dimensions={0}, use_global_device_ids=true | all-gather | bytes 589824 | tf_op jit(solution)/shard_map/all_gather | solution.py:13
  151.0 25.0 %all-reduce.19.cloned.1.call-done = f32[128,128]{0,1:T(8,128)} async-done(((f32[128,128]{0,1:T(8,128)}), f32[128,128]{0,1:T(8,128)}) %all-reduce.19.cloned.1.call-update) | async-done | bytes 65552 | tf_op jit(solution)/shard_map/psum | solution.py:94
  176.0 1.1 fusion.124
  177.3 0.3 convolution_add_fusion.12
  177.6 0.3 convolution_add_fusion.11
  177.8 0.3 convolution_add_fusion.10
  178.1 0.3 convolution_add_fusion.9
  178.4 0.3 convolution_add_fusion.8
  178.7 0.3 convolution_add_fusion.7
  179.0 8.8 %all-gather.2 = f32[8,1,128]{2,1,0:T(1,128)S(1)} all-gather(f32[1,1,128]{2,1,0:T(1,128)S(1)} %slice_bitcast_fusion.1), channel_id=1, replica_groups=mesh['tm'=8,'sr'=4] {'tm'}, dimensions={0}, use_global_device_ids=true | all-gather | bytes 4608 | tf_op jit(solution)/shard_map/all_gather | solution.py:13
  188.2 0.2 fusion.73
  188.5 0.2 fusion.57
  189.3 0.2 fusion.135
  189.5 0.3 fusion.12
  189.9 0.3 convolution_add_fusion.6
  190.1 0.3 convolution_add_fusion.5
  190.4 0.3 convolution_add_fusion.4
  190.7 0.3 convolution_add_fusion.3
  191.0 0.3 convolution_add_fusion.2
  191.3 0.3 convolution_add_fusion.1
  191.5 0.3 convolution_add_fusion
  191.8 9.7 %all-gather.3 = f32[8,1,128]{2,1,0:T(1,128)S(1)} all-gather(f32[1,1,128]{2,1,0:T(1,128)S(1)} %slice_bitcast_fusion), channel_id=1, replica_groups=mesh['tm'=8,'sr'=4] {'tm'}, dimensions={0}, use_global_device_ids=true | all-gather | bytes 4608 | tf_op jit(solution)/shard_map/all_gather | solution.py:13
  201.5 1.6 while.27
  201.7 0.2 fusion.247
  201.9 0.2 fusion.247
  202.2 0.2 fusion.247
  202.4 0.2 fusion.247
  202.6 0.2 fusion.247
  202.8 0.2 fusion.247
  203.1 0.2 fusion.95
  203.3 0.2 fusion.93
  203.5 0.2 fusion.89
  203.7 0.2 fusion.79
  204.0 0.2 fusion.65
  204.8 0.2 fusion.146
  205.1 1.0 fusion.36
  206.1 0.9 fusion.147
  207.0 2.0 collective-permute-start
  209.0 8.7 %all_gather.27 = bf16[1024,128]{1,0:T(8,128)(2,1)S(1)} all-gather(bf16[128,128]{1,0:T(8,128)(2,1)S(1)} %get-tuple-element.157), channel_id=1, replica_groups=mesh['tm'=8,'sr'=4] {'tm'}, dimensions={0}, use_global_device_ids=true | all-gather | bytes 294912 | tf_op jit(solution)/shard_map/all_gather | solution.py:129
  217.7 0.9 fusion.21
  218.7 2.9 fusion.148
  221.6 49.8 %all-reduce.23.cloned.1.call-done = (f32[128,128]{0,1:T(8,128)}, f32[128,128]{0,1:T(8,128)}, f32[128,128]{0,1:T(8,128)}) async-done(((f32[128,128]{0,1:T(8,128)}, f32[128,128]{0,1:T(8,128)}, f32[128,128]{0,1:T(8,128)}), (f32[128,128]{0,1:T(8,128)}, f32[128,128]{0,1:T(8,128)}, f32[128,128]{0,1:T(8,128)})) %all-reduce.23.cloned.1.call-update) | async-done | bytes 196624 | tf_op jit(solution)/shard_map/psum | solution.py:120
  271.4 0.9 multiply_add_fusion
  272.5 11.7 %cholesky.55 = f32[128,128]{1,0:T(8,128)S(1)} custom-call(f32[128,128]{1,0:T(8,128)S(1)} %get-tuple-element.161), custom_call_target="Cholesky" | custom-call | tf_op jit(solution)/shard_map/jit(cholesky)/cholesky | solution.py:134
  284.3 0.6 compare_reduce_fusion
  284.9 0.7 fusion.20
  285.6 9.8 %custom-call.17 = f32[1,128,128]{1,2,0:T(8,128)S(1)} custom-call(f32[1,128,128]{2,1,0:T(8,128)S(1)} %fusion.20), custom_call_target="InvertDiagBlocksLowerTriangular" | custom-call | tf_op jit(solution)/shard_map/jit(_cho_solve)/triangular_solve | solution.py:135
  295.4 1.1 fusion.27
  296.5 0.9 fusion.25
  297.4 11.7 %cholesky.44 = f32[128,128]{1,0:T(8,128)S(1)} custom-call(f32[128,128]{1,0:T(8,128)S(1)} %get-tuple-element.162), custom_call_target="Cholesky" | custom-call | tf_op jit(solution)/shard_map/jit(cholesky)/cholesky | solution.py:132
  309.2 0.6 compare_reduce_fusion.1
  309.8 0.7 fusion.19
  310.5 9.9 %custom-call.16 = f32[1,128,128]{1,2,0:T(8,128)S(1)} custom-call(f32[1,128,128]{2,1,0:T(8,128)S(1)} %fusion.19), custom_call_target="InvertDiagBlocksLowerTriangular" | custom-call | tf_op jit(solution)/shard_map/jit(_cho_solve)/triangular_solve | solution.py:133
  320.5 1.1 fusion.32
  321.5 2.8 fusion.30
  (87 shorter events, 6.0 us)
Async XLA Ops:
  8.0 10.0 %copy-start = (f32[128,128]{1,0:T(8,128)S(1)}, f32[128,128]{1,0:T(8,128)}, u32[]{:S(2)}) copy-start(f32[128,128]{1,0:T(8,128)} %param.17) | copy-start | bytes 196612
  8.0 9.9 %copy-start.2 = (f32[128,128]{1,0:T(8,128)S(1)}, f32[128,128]{1,0:T(8,128)}, u32[]{:S(2)}) copy-start(f32[128,128]{1,0:T(8,128)} %param.15) | copy-start | bytes 196612
  8.0 10.4 %copy-start.3 = (f32[128,128]{1,0:T(8,128)S(1)}, f32[128,128]{1,0:T(8,128)}, u32[]{:S(2)}) copy-start(f32[128,128]{1,0:T(8,128)} %param.18) | copy-start | bytes 196612
  8.0 129.3 %all-reduce.21.cloned.1.call-start = ((), (), s32[]{:S(2)}) async-start(), calls=%async_computation.3 | async-start | bytes 131072 | tf_op jit(solution)/shard_map/psum | solution.py:95
  12.5 126.0 %copy-start.4 = (f32[128,128]{1,0:T(8,128)S(1)}, f32[128,128]{1,0:T(8,128)}, u32[]{:S(2)}) copy-start(f32[128,128]{1,0:T(8,128)} %param.16) | copy-start | bytes 196612
  12.5 128.0 %reduce-scatter.2.cloned.1.call-start = ((), (), s32[]{:S(2)}) async-start(), calls=%async_computation.1 | async-start | bytes 589824 | tf_op jit(solution)/shard_map/reduce_scatter | solution.py:87
  17.9 158.1 %all-reduce.19.cloned.1.call-start = ((), (), s32[]{:S(2)}) async-start(), calls=%async_computation.2 | async-start | bytes 131072 | tf_op jit(solution)/shard_map/psum | solution.py:94
  140.6 130.9 %all-reduce.23.cloned.1.call-start = ((), (), s32[]{:S(2)}) async-start(), calls=%async_computation.4 | async-start | bytes 393216 | tf_op jit(solution)/shard_map/psum | solution.py:120
  205.1 105.4 %copy-start.1 = (f32[128,128]{1,0:T(8,128)}, f32[128,128]{1,0:T(8,128)S(1)}, u32[]{:S(2)}) copy-start(f32[128,128]{1,0:T(8,128)S(1)} %get-tuple-element.158) | copy-start | bytes 196612
  207.0 10.7 %collective-permute-start = (f32[1,128]{1,0:T(1,128)S(1)}, f32[1,128]{1,0:T(1,128)S(1)}, u32[]{:S(2)}, u32[]{:S(2)}) collective-permute-start(f32[1,128]{1,0:T(1,128)S(1)} %slice.121), channel_id=1, source_target_pairs={{0,4},{4,8},{8,12},{12,16},{16,20},{20,24},{24,28},{1,5},{5,9},{9,... | collective-permute-start | bytes 1544 | tf_op jit(solution)/shard_map/ppermute | solution.py:28
Sparse Core Ops, SparseCore 0:
  15.0 122.2 all-reduce.20
Sparse Core Ops, SparseCore 1:
  18.0 36.8 reduce-scatter.1
  140.6 35.2 all-reduce.18
  218.7 52.6 all-reduce.22
where the time goes:
time: 332 us
  waiting for transfers between devices  181 us (55%)
  blocking collectives  48.9 us (15%)
  other arithmetic  46.8 us (14%)
  matrix products  36.4 us (11%)
  between operations  16.2 us (5%)
    psum x1, waiting for transfers between devices, local(): info = lax.psum(info_part, ('tm', 'sr'))  106 us
    psum x1, waiting for transfers between devices, local(): lax.psum((total_part, previous_part, lagged_part), 'tm')  49.8 us
    all_gather x4, blocking collectives, carried_in(): gathered = jax.tree.map(lambda a: lax.all_gather(a, axis), part)  40.2 us
    psum x1, waiting for transfers between devices, local(): proj = lax.psum(partial_value, 'sr')  25 us
    dot_general x63, matrix products, dot_high(): jnp.dot(left, right, precision=precise, preferred_element_type=jnp.float32)  22.3 us
    another operation x3, other arithmetic, local(): previous_factor = jnp.linalg.cholesky(previous)  12.4 us
    another operation x3, other arithmetic, local(): total_factor = jnp.linalg.cholesky(total)  12.4 us
    another operation x2, other arithmetic, local(): new_loadings = jax.scipy.linalg.cho_solve((total_factor, True), cross.T).T  10.6 us
  transfers between devices with their start and end apart: 5, of which 3 were waited for; matrix products, arithmetic and copies ran while one was open for 4% of the time, Pallas kernels for 0%

commit v1 on v0

--- a/solution.py
+++ b/solution.py
@@ -91,7 +91,8 @@
         tiled=True,
     )
     info_part = dot_high(loadings.T, noise_precision[:, None] * loadings)
-    proj = lax.psum(partial_value, "sr")
+    terms = lax.all_gather(partial_value, "sr", axis=0, tiled=False)
+    proj = terms.sum(axis=0)
     info = lax.psum(info_part, ("tm", "sr"))
     closed = transition - dot_high(filter_cov, dot_high(info, transition))
     inputs = dot_high(proj, filter_cov.T)

time: 332 us -> 321 us (0.967)
  waiting for transfers between devices: 181 us -> 156 us
  blocking collectives: 48.9 us -> 63.2 us
    psum x1 -> x0, waiting for transfers between devices: 25 us -> none  [local(): proj = lax.psum(partial_value, 'sr')]
    all_gather x0 -> x1, blocking collectives: none -> 14.3 us  [local(): terms = lax.all_gather(partial_value, 'sr', axis=0, tiled=False)]
  transfers between devices with their start and end apart: 5 -> 4, of which waited for: 3 -> 2; matrix products, arithmetic and copies ran while one was open for 4% -> 4% of each run, Pallas kernels for 0% -> 0%
where the time goes in v1:
time: 321 us; the launch traced here: 320 us
  waiting for transfers between devices  156 us (49%)
  blocking collectives  63.2 us (20%)
  other arithmetic  46.9 us (15%)
  matrix products  35.5 us (11%)
  between operations  16 us (5%)
    psum x1, waiting for transfers between devices, local(): info = lax.psum(info_part, ('tm', 'sr'))  106 us
    psum x1, waiting for transfers between devices, local(): lax.psum((total_part, previous_part, lagged_part), 'tm')  49.8 us
    all_gather x4, blocking collectives, carried_in(): gathered = jax.tree.map(lambda a: lax.all_gather(a, axis), part)  39.8 us
    dot_general x63, matrix products, dot_high(): jnp.dot(left, right, precision=precise, preferred_element_type=jnp.float32)  21.5 us
    all_gather x1, blocking collectives, local(): terms = lax.all_gather(partial_value, 'sr', axis=0, tiled=False)  14.3 us
    another operation x3, other arithmetic, local(): previous_factor = jnp.linalg.cholesky(previous)  12.4 us
    another operation x3, other arithmetic, local(): total_factor = jnp.linalg.cholesky(total)  12.4 us
    another operation x2, other arithmetic, local(): new_loadings = jax.scipy.linalg.cho_solve((total_factor, True), cross.T).T  10.6 us
  transfers between devices with their start and end apart: 4, of which 2 were waited for; matrix products, arithmetic and copies ran while one was open for 4% of the time, Pallas kernels for 0%

profile of v1, /device:TPU:0, one launch (start us, length us, event | category | flops | bytes accessed | tf_op | source)
XLA Modules:
  0.0 320.5 jit_solution(1106146978165982557)
XLA Ops:
  8.1 4.4 %fusion.13 = f32[128,128]{0,1:T(8,128)} fusion(f32[2048,128]{1,0:T(8,128)} %param.13, f32[2048]{0:T(1024)} %param.14), kind=kOutput, calls=%fused_computation.18 | convolution fusion | flops 402915328 | bytes 1122304 | tf_op jit(solution)/shard_map/dot_general | solution.py:32
  12.6 5.3 %convolution_bitcast_fusion.2 = f32[1024,128]{0,1:T(8,128)} fusion(bf16[1024,2048]{1,0:T(8,128)(2,1)} %param.12, f32[2048,128]{1,0:T(8,128)} %param.13, f32[2048]{0:T(1024)} %param.14), kind=kOutput, calls=%fused_computation.15 | convolution fusion | flops 537395200 | bytes 5775360 | tf_op jit(solution)/shard_map/dot_general | solution.py:88
  18.6 0.3 convolution_multiply_fusion
  20.3 11.4 %all-gather.2 = f32[1024,128]{1,0:T(8,128)S(1)} all-gather(f32[128,128]{1,0:T(8,128)S(1)} %fusion.46), channel_id=4, replica_groups=mesh['tm'=8,'sr'=4] {'tm'}, dimensions={0}, use_global_device_ids=true | all-gather | bytes 589824 | tf_op jit(solution)/shard_map/all_gather | solution.py:13
  31.7 105.7 %all-reduce.18.cloned.1.call-done = f32[128,128]{0,1:T(8,128)} async-done(((f32[128,128]{0,1:T(8,128)}), f32[128,128]{0,1:T(8,128)}) %all-reduce.18.cloned.1.call-update) | async-done | bytes 65552 | tf_op jit(solution)/shard_map/psum | solution.py:96
  137.3 1.1 fusion.125
  138.5 0.3 fusion.16
  138.8 0.3 fusion.126
  140.5 10.4 %all-gather.1 = f32[1024,128]{1,0:T(8,128)S(1)} all-gather(f32[128,128]{1,0:T(8,128)S(1)} %fusion.47), channel_id=3, replica_groups=mesh['tm'=8,'sr'=4] {'tm'}, dimensions={0}, use_global_device_ids=true | all-gather | bytes 589824 | tf_op jit(solution)/shard_map/all_gather | solution.py:13
  150.9 14.3 %all-gather = f32[512,128]{0,1:T(8,128)S(1)} all-gather(f32[128,128]{0,1:T(8,128)} %reduce-scatter.2.cloned.1.call-done), channel_id=2, replica_groups=mesh['tm'=8,'sr'=4] {'sr'}, dimensions={0}, use_global_device_ids=true | all-gather | bytes 327680 | tf_op jit(solution)/shard_map/all_gather | solution.py:94
  165.5 0.3 fusion.124
  165.8 0.2 convolution_add_fusion.13
  166.0 0.3 convolution_add_fusion.12
  166.3 0.3 convolution_add_fusion.11
  166.6 0.3 convolution_add_fusion.10
  166.8 0.3 convolution_add_fusion.9
  167.1 0.3 convolution_add_fusion.8
  167.4 0.3 convolution_add_fusion.7
  167.7 8.8 %all-gather.3 = f32[8,1,128]{2,1,0:T(1,128)S(1)} all-gather(f32[1,1,128]{2,1,0:T(1,128)S(1)} %slice_bitcast_fusion.1), channel_id=1, replica_groups=mesh['tm'=8,'sr'=4] {'tm'}, dimensions={0}, use_global_device_ids=true | all-gather | bytes 4608 | tf_op jit(solution)/shard_map/all_gather | solution.py:13
  177.0 0.2 fusion.73
  177.2 0.2 fusion.57
  178.0 0.2 fusion.135
  178.3 0.3 fusion.12
  178.6 0.3 convolution_add_fusion.6
  178.9 0.3 convolution_add_fusion.5
  179.2 0.3 convolution_add_fusion.4
  179.5 0.3 convolution_add_fusion.3
  179.7 0.3 convolution_add_fusion.2
  180.0 0.3 convolution_add_fusion.1
  180.3 0.3 convolution_add_fusion
  180.6 9.2 %all-gather.4 = f32[8,1,128]{2,1,0:T(1,128)S(1)} all-gather(f32[1,1,128]{2,1,0:T(1,128)S(1)} %slice_bitcast_fusion), channel_id=1, replica_groups=mesh['tm'=8,'sr'=4] {'tm'}, dimensions={0}, use_global_device_ids=true | all-gather | bytes 4608 | tf_op jit(solution)/shard_map/all_gather | solution.py:13
  189.8 1.6 while.27
  190.0 0.2 fusion.247
  190.2 0.2 fusion.247
  190.5 0.2 fusion.247
  190.7 0.2 fusion.247
  190.9 0.2 fusion.247
  191.2 0.2 fusion.247
  191.4 0.2 fusion.95
  191.6 0.2 fusion.93
  191.8 0.2 fusion.89
  192.0 0.2 fusion.79
  192.3 0.2 fusion.65
  193.1 0.2 fusion.146
  193.4 1.0 fusion.36
  194.4 0.9 fusion.147
  195.3 2.0 collective-permute-start
  197.3 9.1 %all_gather.35 = bf16[1024,128]{1,0:T(8,128)(2,1)S(1)} all-gather(bf16[128,128]{1,0:T(8,128)(2,1)S(1)} %get-tuple-element.157), channel_id=1, replica_groups=mesh['tm'=8,'sr'=4] {'tm'}, dimensions={0}, use_global_device_ids=true | all-gather | bytes 294912 | tf_op jit(solution)/shard_map/all_gather | solution.py:130
  206.5 0.9 fusion.21
  207.4 2.9 fusion.148
  210.3 49.8 %all-reduce.20.cloned.1.call-done = (f32[128,128]{0,1:T(8,128)}, f32[128,128]{0,1:T(8,128)}, f32[128,128]{0,1:T(8,128)}) async-done(((f32[128,128]{0,1:T(8,128)}, f32[128,128]{0,1:T(8,128)}, f32[128,128]{0,1:T(8,128)}), (f32[128,128]{0,1:T(8,128)}, f32[128,128]{0,1:T(8,128)}, f32[128,128]{0,1:T(8,128)})) %all-reduce.20.cloned.1.call-update) | async-done | bytes 196624 | tf_op jit(solution)/shard_map/psum | solution.py:121
  260.1 0.9 multiply_add_fusion
  261.3 11.7 %cholesky.55 = f32[128,128]{1,0:T(8,128)S(1)} custom-call(f32[128,128]{1,0:T(8,128)S(1)} %get-tuple-element.161), custom_call_target="Cholesky" | custom-call | tf_op jit(solution)/shard_map/jit(cholesky)/cholesky | solution.py:135
  273.0 0.6 compare_reduce_fusion
  273.6 0.7 fusion.20
  274.3 9.8 %custom-call.17 = f32[1,128,128]{1,2,0:T(8,128)S(1)} custom-call(f32[1,128,128]{2,1,0:T(8,128)S(1)} %fusion.20), custom_call_target="InvertDiagBlocksLowerTriangular" | custom-call | tf_op jit(solution)/shard_map/jit(_cho_solve)/triangular_solve | solution.py:136
  284.1 1.1 fusion.27
  285.3 0.9 fusion.25
  286.2 11.7 %cholesky.44 = f32[128,128]{1,0:T(8,128)S(1)} custom-call(f32[128,128]{1,0:T(8,128)S(1)} %get-tuple-element.162), custom_call_target="Cholesky" | custom-call | tf_op jit(solution)/shard_map/jit(cholesky)/cholesky | solution.py:133
  297.9 0.6 compare_reduce_fusion.1
  298.6 0.7 fusion.19
  299.2 9.9 %custom-call.16 = f32[1,128,128]{1,2,0:T(8,128)S(1)} custom-call(f32[1,128,128]{2,1,0:T(8,128)S(1)} %fusion.19), custom_call_target="InvertDiagBlocksLowerTriangular" | custom-call | tf_op jit(solution)/shard_map/jit(_cho_solve)/triangular_solve | solution.py:134
  309.2 1.1 fusion.32
  310.2 2.8 fusion.30
  (87 shorter events, 6.2 us)
Async XLA Ops:
  8.0 10.0 %copy-start = (f32[128,128]{1,0:T(8,128)S(1)}, f32[128,128]{1,0:T(8,128)}, u32[]{:S(2)}) copy-start(f32[128,128]{1,0:T(8,128)} %param.17) | copy-start | bytes 196612
  8.0 9.9 %copy-start.2 = (f32[128,128]{1,0:T(8,128)S(1)}, f32[128,128]{1,0:T(8,128)}, u32[]{:S(2)}) copy-start(f32[128,128]{1,0:T(8,128)} %param.15) | copy-start | bytes 196612
  8.0 10.4 %copy-start.3 = (f32[128,128]{1,0:T(8,128)S(1)}, f32[128,128]{1,0:T(8,128)}, u32[]{:S(2)}) copy-start(f32[128,128]{1,0:T(8,128)} %param.18) | copy-start | bytes 196612
  8.0 129.3 %all-reduce.18.cloned.1.call-start = ((), (), s32[]{:S(2)}) async-start(), calls=%async_computation.2 | async-start | bytes 131072 | tf_op jit(solution)/shard_map/psum | solution.py:96
  12.5 126.0 %copy-start.4 = (f32[128,128]{1,0:T(8,128)S(1)}, f32[128,128]{1,0:T(8,128)}, u32[]{:S(2)}) copy-start(f32[128,128]{1,0:T(8,128)} %param.16) | copy-start | bytes 196612
  12.5 138.4 %reduce-scatter.2.cloned.1.call-start = ((), (), s32[]{:S(2)}) async-start(), calls=%async_computation.1 | async-start | bytes 589824 | tf_op jit(solution)/shard_map/reduce_scatter | solution.py:87
  17.9 242.3 %all-reduce.20.cloned.1.call-start = ((), (), s32[]{:S(2)}) async-start(), calls=%async_computation.3 | async-start | bytes 393216 | tf_op jit(solution)/shard_map/psum | solution.py:121
  193.4 105.9 %copy-start.1 = (f32[128,128]{1,0:T(8,128)}, f32[128,128]{1,0:T(8,128)S(1)}, u32[]{:S(2)}) copy-start(f32[128,128]{1,0:T(8,128)S(1)} %get-tuple-element.158) | copy-start | bytes 196612
  195.3 11.2 %collective-permute-start = (f32[1,128]{1,0:T(1,128)S(1)}, f32[1,128]{1,0:T(1,128)S(1)}, u32[]{:S(2)}, u32[]{:S(2)}) collective-permute-start(f32[1,128]{1,0:T(1,128)S(1)} %slice.121), channel_id=1, source_target_pairs={{0,4},{4,8},{8,12},{12,16},{16,20},{20,24},{24,28},{1,5},{5,9},{9,... | collective-permute-start | bytes 1544 | tf_op jit(solution)/shard_map/ppermute | solution.py:28
Sparse Core Ops, SparseCore 0:
  15.0 122.2 all-reduce.17
Sparse Core Ops, SparseCore 1:
  18.0 36.8 reduce-scatter.1
  207.5 52.6 all-reduce.19
